TPU v7x, 32 devices: a whole 2x2x4 slice. The times are simulated.
32 devices in a mesh: dom: 8 (over y, x, core), col: 4 (over z).
Axes of the slice: x: 2, y: 2, z: 4, core: 2. Of those that a mesh axis runs over, the one named last changes fastest.
Arguments:
- features: bfloat16 [65536, 1024], P('dom', 'col')
- weight: bfloat16 [1024, 1024], P(None, 'col'), may hold values from -0.1875 to 0.1875
- out_bias: bfloat16 [1024], P('col'), may hold values from -3 to 3
- local_index: int32 [8, 64, 4], P('dom'), may hold values from 0 to 63
- local_count: int32 [8, 64], P('dom'), may hold values from 1 to 4, as said below
- local_vals: bfloat16 [8, 64, 4, 128, 128], P('dom'), may hold values from -0.1875 to 0.1875
- halo_index: int32 [8, 64, 4], P('dom'), may hold values from 0 to 31
- halo_count: int32 [8, 64], P('dom'), may hold values from 0 to 4, as said below
- halo_vals: bfloat16 [8, 64, 4, 128, 128], P('dom'), may hold values from -0.1875 to 0.1875
- send_rows: int32 [8, 8, 512], P('dom'), may hold values from 0 to 8191
- send_count: int32 [8, 8], P('dom'), may hold values from 0 to 512, as said below
Outputs:
- normalized: bfloat16 [65536, 1024], P('dom', 'col')
- channel_stats: float32 [2, 1024], P(None, 'col')
Inputs may be any that keep to these rules, and one draw needn't show every extreme that they name: `local_index`: slots k >= local_count of a row tile are not used. `local_count`: every partition has a row tile with all 4 slots used. `halo_index`: slots k >= halo_count of a row tile are not used. `halo_count`: every partition has a row tile with all 4 slots used. `send_rows`: slots s >= send_count[q, p] are not used. send_count[p, p] is 0; every partition fills all 512 slots to some other partition.
All inputs are finite; a program needn't handle non-finite values.
Results may differ from a plain program's by a relative error of at most 0.0075.
Values may be sent and summed in bfloat16 or wider, within the bound.
A program may use at most 192 MiB of HBM per device.

v0:
```python
import jax
import jax.numpy as jnp
from jax import lax
from jax.sharding import PartitionSpec as P

TILE = 128


epsilon = 1e-06


def tile_sum(sources, tile_index, tile_count, tile_vals):
    gathered = sources[tile_index]
    keep_mask = jnp.arange(tile_vals.shape[1])[None, :] < tile_count[:, None]
    masked = jnp.where(keep_mask[:, :, None, None], tile_vals, jnp.zeros_like(tile_vals))
    return jnp.einsum("tkij,tkjc->tic", masked, gathered, preferred_element_type=jnp.float32)


def on_device(
    features,
    weight,
    out_bias,
    local_index,
    local_count,
    local_vals,
    halo_index,
    halo_count,
    halo_vals,
    send_rows,
    send_count,
):
    row_count, col_width = features.shape
    peer_count = lax.axis_size("dom")
    slot_total = send_rows.shape[2]
    chosen = features[send_rows[0]]
    keep_mask = jnp.arange(slot_total)[None, :] < send_count[0][:, None]
    outgoing = jnp.where(keep_mask[:, :, None], chosen, jnp.zeros_like(chosen))
    arrived = lax.all_to_all(outgoing, "dom", split_axis=0, concat_axis=0, tiled=True)
    halo_tiles = arrived.reshape(peer_count * slot_total // TILE, TILE, col_width)
    own_tiles = features.reshape(row_count // TILE, TILE, col_width)
    summed = tile_sum(own_tiles, local_index[0], local_count[0], local_vals[0])
    summed = summed + tile_sum(halo_tiles, halo_index[0], halo_count[0], halo_vals[0])
    spread = summed.reshape(row_count, col_width).astype(jnp.bfloat16)
    node_total = row_count * peer_count
    regrouped = lax.all_to_all(spread, "col", split_axis=0, concat_axis=1, tiled=True)
    full_weight, full_bias = (
        lax.all_gather(weight, "col", axis=1, tiled=True),
        lax.all_gather(out_bias.reshape(1, col_width), "col", axis=1, tiled=True),
    )
    mixed_rows = jnp.dot(regrouped, full_weight, preferred_element_type=jnp.float32) + full_bias[
        0
    ].astype(jnp.float32)
    active = jnp.maximum(mixed_rows, 0.0)
    row_power = jnp.mean(active * active, axis=1, keepdims=True)
    scaled = active * lax.rsqrt(row_power + epsilon)
    sum_whole, square_whole = lax.psum(
        (jnp.sum(scaled, axis=0), jnp.sum(scaled * scaled, axis=0)), ("dom", "col")
    )
    normalized = lax.all_to_all(
        scaled.astype(jnp.bfloat16), "col", split_axis=1, concat_axis=0, tiled=True
    )
    column_start = lax.axis_index("col") * col_width
    sum_total = lax.dynamic_slice_in_dim(sum_whole, column_start, col_width, 0)
    square_total = lax.dynamic_slice_in_dim(square_whole, column_start, col_width, 0)
    channel_mean = sum_total / node_total
    channel_var = square_total / node_total - channel_mean * channel_mean
    return (normalized, jnp.stack([channel_mean, channel_var]))


def solution(mesh):
    in_specs = (
        P("dom", "col"),
        P(None, "col"),
        P("col"),
        P("dom", None, None),
        P("dom", None),
        P("dom", None, None, None, None),
        P("dom", None, None),
        P("dom", None),
        P("dom", None, None, None, None),
        P("dom", None, None),
        P("dom", None),
    )
    out_specs = (P("dom", "col"), P(None, "col"))
    return jax.shard_map(
        on_device, mesh=mesh, in_specs=in_specs, out_specs=out_specs, check_vma=False
    )
```

profile of v0, /device:TPU:0, one launch (start us, length us, event | category | flops | bytes accessed | tf_op | source)
XLA Modules:
  0.0 374.6 jit_solution(2426596609186330712)
XLA Ops:
  7.2 0.7 fusion.10
  7.9 0.7 iota_compare_fusion.2
  8.6 15.7 %gather_fusion.1 = bf16[4096,256]{1,0:T(8,128)(2,1)S(1)} fusion(bf16[8192,256]{1,0:T(8,128)(2,1)} %param.11, s32[4096]{0:T(1024)S(1)} %broadcast_clamp_fusion), kind=kCustom, calls=%fused_computation.1 | custom fusion | bytes 4210688 | tf_op jit(solution)/shard_map/gather | solution.py:35
  24.4 0.0 copy-start
  24.4 0.0 copy-start.1
  24.4 1.7 broadcast_select_fusion
  26.1 5.2 %all-to-all-start = ((bf16[8,512,256]{2,1,0:T(8,128)(2,1)}), bf16[8,512,256]{2,1,0:T(8,128)(2,1)S(1)}, u32[]{:S(2)}, u32[]{:S(2)}) async-start(bf16[8,512,256]{2,1,0:T(8,128)(2,1)} %broadcast_select_fusion), calls=%async_computation | async-start | bytes 4194304 | tf_op jit(solution)/shard_map/all_to_all | solution.py:38
  31.3 0.1 copy.19
  31.4 0.1 reshape.208
  31.5 0.1 copy.18
  31.6 0.1 reshape.192
  31.7 0.0 copy-start.3
  31.7 12.0 %gather_fusion = bf16[256,128,256]{2,1,0:T(8,128)(2,1)} fusion(bf16[64,128,256]{2,1,0:T(8,128)(2,1)} %bitcast.52, s32[1024]{0:T(1024)S(1)} %pad_clamp_fusion.1), kind=kCustom, calls=%fused_computation | custom fusion | bytes 33555456 | tf_op jit(solution)/shard_map/gather | solution.py:13
  43.7 0.1 iota_compare_fusion
  43.8 0.1 iota_compare_fusion.1
  43.9 14.0 %all-to-all-done = bf16[8,512,256]{2,1,0:T(8,128)(2,1)S(1)} async-done(((bf16[8,512,256]{2,1,0:T(8,128)(2,1)}), bf16[8,512,256]{2,1,0:T(8,128)(2,1)S(1)}, u32[]{:S(2)}, u32[]{:S(2)}) %all-to-all-start) | async-done | bytes 2097184 | tf_op jit(solution)/shard_map/all_to_all | solution.py:38
  57.9 9.8 %gather_fusion.2 = bf16[256,128,256]{2,1,0:T(8,128)(2,1)} fusion(bf16[32,128,256]{2,1,0:T(8,128)(2,1)S(1)} %bitcast.53, s32[1024]{0:T(1024)S(1)} %pad_clamp_fusion), kind=kCustom, calls=%fused_computation.2 | custom fusion | bytes 33555456 | tf_op jit(solution)/shard_map/gather | solution.py:13
  67.6 13.8 %fusion.1 = f32[64,128,256,1]{2,1,3,0:T(8,128)} fusion(bf16[64,4,128,256]{3,2,1,0:T(8,128)(2,1)} %bitcast.54, bf16[1,64,4,128,128]{4,3,2,1,0:T(8,128)(2,1)} %param.19, pred[64,4]{1,0:T(8,128)(4,1)S(1)} %iota_compare_fusion), kind=kOutput, calls=%fused_computation.6 | convolution fusion | flops 2151677952 | bytes 33554688 | tf_op jit(solution)/shard_map/tkij,tkjc->tic/dot_general | solution.py:16
  81.4 14.0 %fusion = bf16[64,128,256]{2,1,0:T(8,128)(2,1)} fusion(f32[64,128,256,1]{2,1,3,0:T(8,128)} %fusion.1, bf16[64,4,128,256]{3,2,1,0:T(8,128)(2,1)} %bitcast.55, bf16[1,64,4,128,128]{4,3,2,1,0:T(8,128)(2,1)} %param.16, pred[64,4]{1,0:T(8,128)(4,1)S(1)} %iota_compare_fusion.1), kind=kOutput, calls=%fused_computation.4 | convolution fusion | flops 2155872256 | bytes 37748992 | tf_op jit(solution)/shard_map/tkij,tkjc->tic/dot_general | solution.py:16
  95.4 6.3 %copy.20 = bf16[4,2048,256]{1,2,0:T(8,128)(2,1)} copy(bf16[4,2048,256]{2,1,0:T(8,128)(2,1)} %bitcast.56) | data formatting | bytes 8388608 | tf_op jit(solution)/shard_map/convert_element_type | solution.py:43
  101.6 4.9 %all-to-all-start.1 = ((bf16[4,2048,256]{1,2,0:T(8,128)(2,1)}), bf16[4,2048,256]{1,2,0:T(8,128)(2,1)}, u32[]{:S(2)}, u32[]{:S(2)}) async-start(bf16[4,2048,256]{1,2,0:T(8,128)(2,1)} %copy.20), calls=%async_computation.1 | async-start | bytes 8388608 | tf_op jit(solution)/shard_map/all_to_all | solution.py:45
  106.5 0.0 all-gather.4.cloned.1.call-start
  106.5 0.7 all-gather.4.cloned.1.call-update
  107.3 103.9 %all-gather.1 = bf16[4,1,256]{2,1,0:T(2,128)(2,1)S(1)} all-gather(bf16[1,1,256]{2,1,0:T(2,128)(2,1)S(1)} %reshape.220), channel_id=2, replica_groups=mesh['dom'=8,'col'=4] {'col'}, dimensions={0}, use_global_device_ids=true | all-gather | bytes 2560 | tf_op jit(solution)/shard_map/all_gather | solution.py:48
  211.2 19.8 %all-to-all-done.1 = bf16[4,2048,256]{1,2,0:T(8,128)(2,1)} async-done(((bf16[4,2048,256]{1,2,0:T(8,128)(2,1)}), bf16[4,2048,256]{1,2,0:T(8,128)(2,1)}, u32[]{:S(2)}, u32[]{:S(2)}) %all-to-all-start.1) | async-done | bytes 4194336 | tf_op jit(solution)/shard_map/all_to_all | solution.py:45
  231.0 7.8 %multiply_reduce_fusion.1 = (f32[2048]{0:T(1024)S(1)}, f32[2048,1024]{0,1:T(8,128)S(1)}) fusion(f32[1024]{0:T(1024)S(1)} %bitcast.61, bf16[2048,1024]{0,1:T(8,128)(2,1)} %bitcast.19, bf16[1024,1024]{1,0:T(8,128)(2,1)} %all-gather.4.cloned.1.call-done), kind=kOutput, calls=%fused_computation.10 | convolution fusion | flops 4303353856 | bytes 14692352 | tf_op jit(solution)/shard_map/dot_general | solution.py:50
  238.7 3.5 fusion.6
  242.2 4.8 %all-to-all-start.2 = ((bf16[2048,4,256]{0,2,1:T(8,128)(2,1)}), bf16[2048,4,256]{0,2,1:T(8,128)(2,1)}, u32[]{:S(2)}, u32[]{:S(2)}) async-start(bf16[2048,4,256]{0,2,1:T(8,128)(2,1)} %bitcast.57), calls=%async_computation.2 | async-start | bytes 8388608 | tf_op jit(solution)/shard_map/all_to_all | solution.py:59
  247.1 113.8 %all-reduce = (f32[1024]{0:T(1024)S(1)}, f32[1024]{0:T(1024)S(1)}) all-reduce(f32[1024]{0:T(1024)S(1)} %get-tuple-element.3, f32[1024]{0:T(1024)S(1)} %get-tuple-element.2), channel_id=1, replica_groups=mesh['dom'=8,'col'=4] {'dom','col'}, use_global_device_ids=true, to_apply=%region_4.5 | all-reduce | flops 2048 | bytes 16384 | tf_op jit(solution)/shard_map/psum | solution.py:56
  360.9 0.1 dynamic-slice_multiply_fusion
  361.0 0.6 pad_maximum_fusion
  361.6 6.2 %copy.21 = bf16[4,2048,256]{2,1,0:T(8,128)(2,1)} copy(bf16[4,2048,256]{1,2,0:T(8,128)(2,1)} %bitcast.22) | data formatting | bytes 8388608 | tf_op jit(solution)/shard_map/all_to_all | solution.py:59
  (18 shorter events, 0.1 us)
Async XLA Ops:
  24.4 6.9 %copy-start = (s32[1,64,4]{1,2,0:T(4,128)S(1)}, s32[1,64,4]{1,2,0:T(4,128)}, u32[]{:S(2)}) copy-start(s32[1,64,4]{1,2,0:T(4,128)} %param.17) | copy-start | bytes 3076
  24.4 7.1 %copy-start.1 = (s32[1,64,4]{1,2,0:T(4,128)S(1)}, s32[1,64,4]{1,2,0:T(4,128)}, u32[]{:S(2)}) copy-start(s32[1,64,4]{1,2,0:T(4,128)} %param.14) | copy-start | bytes 3076
  26.1 31.8 %all-to-all-start = ((bf16[8,512,256]{2,1,0:T(8,128)(2,1)}), bf16[8,512,256]{2,1,0:T(8,128)(2,1)S(1)}, u32[]{:S(2)}, u32[]{:S(2)}) async-start(bf16[8,512,256]{2,1,0:T(8,128)(2,1)} %broadcast_select_fusion), calls=%async_computation | async-start | bytes 4194304 | tf_op jit(solution)/shard_map/all_to_all | solution.py:38
  31.7 12.0 %copy-start.2 = (s32[1,64]{1,0:T(1,128)S(1)}, s32[1,64]{1,0:T(1,128)}, u32[]{:S(2)}) copy-start(s32[1,64]{1,0:T(1,128)} %param.18) | copy-start | bytes 772
  31.7 12.1 %copy-start.3 = (s32[1,64]{1,0:T(1,128)S(1)}, s32[1,64]{1,0:T(1,128)}, u32[]{:S(2)}) copy-start(s32[1,64]{1,0:T(1,128)} %param.15) | copy-start | bytes 772
  95.4 11.9 %copy-start.4 = (bf16[256]{0:T(256)(128)(2,1)S(1)}, bf16[256]{0:T(256)(128)(2,1)}, u32[]{:S(2)}) copy-start(bf16[256]{0:T(256)(128)(2,1)} %param.13) | copy-start | bytes 1540
  101.6 129.3 %all-to-all-start.1 = ((bf16[4,2048,256]{1,2,0:T(8,128)(2,1)}), bf16[4,2048,256]{1,2,0:T(8,128)(2,1)}, u32[]{:S(2)}, u32[]{:S(2)}) async-start(bf16[4,2048,256]{1,2,0:T(8,128)(2,1)} %copy.20), calls=%async_computation.1 | async-start | bytes 8388608 | tf_op jit(solution)/shard_map/all_to_all | solution.py:45
  106.5 104.7 %all-gather.4.cloned.1.call-start = ((), (), s32[]{:S(2)}) async-start(), calls=%async_computation.3 | async-start | bytes 2621440 | tf_op jit(solution)/shard_map/all_gather | solution.py:47
  242.2 119.4 %all-to-all-start.2 = ((bf16[2048,4,256]{0,2,1:T(8,128)(2,1)}), bf16[2048,4,256]{0,2,1:T(8,128)(2,1)}, u32[]{:S(2)}, u32[]{:S(2)}) async-start(bf16[2048,4,256]{0,2,1:T(8,128)(2,1)} %bitcast.57), calls=%async_computation.2 | async-start | bytes 8388608 | tf_op jit(solution)/shard_map/all_to_all | solution.py:59
Sparse Core Ops, SparseCore 0:
  108.9 94.6 all-gather.3
where the time goes:
time: 375 us
  blocking collectives  218 us (58%)
  local copies, waits for them, and re-layouts  50.3 us (13%)
  matrix products  35.5 us (9%)
  waiting for transfers between devices  34.4 us (9%)
  starting transfers between devices  14.9 us (4%)
  between operations  14.2 us (4%)
  other arithmetic  7.48 us (2%)
    psum x1, blocking collectives, on_device(): lax.psum((jnp.sum(scaled, axis=0), jnp.sum(scaled * scaled, axis=0)), ('d...  114 us
    all_gather x1, blocking collectives, on_device(): lax.all_gather(out_bias.reshape(1, col_width), 'col', axis=1, tiled=True)  104 us
    dot_general x2, matrix products, tile_sum(): jnp.einsum('tkij,tkjc->tic', masked, gathered, preferred_element_type=jnp...  27.7 us
    gather x2, local copies, waits for them, and re-layouts, tile_sum(): gathered = sources[tile_index]  21.7 us
    all_to_all x1, waiting for transfers between devices, on_device(): lax.all_to_all(spread, 'col', split_axis=0, concat_axis=1, tiled=True)  19.8 us
    gather x1, local copies, waits for them, and re-layouts, on_device(): chosen = features[send_rows[0]]  15.7 us
    all_to_all x1, waiting for transfers between devices, on_device(): lax.all_to_all(outgoing, 'dom', split_axis=0, concat_axis=0, tiled=True)  14 us
    dot_general x1, matrix products, on_device(): jnp.dot(regrouped, full_weight, preferred_element_type=jnp.float32)  7.76 us
  transfers between devices with their start and end apart: 4, of which 2 were waited for; matrix products, arithmetic and copies ran while one was open for 4% of the time, Pallas kernels for 0%

commit v1 on v0

v1 whole, which is shorter than its diff:
```python
import functools

import jax
import jax.numpy as jnp
from jax import lax
from jax.experimental import pallas as pl
from jax.experimental.pallas import tpu as pltpu
from jax.sharding import PartitionSpec as P

TILE = 128
MESH = pl.DeviceIdType.MESH
CHUNK_TILES = 2
epsilon = 1e-06


def remote(src, dst, send_sem, recv_sem, device):
    return pltpu.make_async_remote_copy(
        src_ref=src,
        dst_ref=dst,
        send_sem=send_sem,
        recv_sem=recv_sem,
        device_id=device,
        device_id_type=MESH,
    )


def kernel(
    n_dom,
    n_col,
    node_total,
    feat_hbm,
    weight_ref,
    bias_ref,
    lidx,
    lcnt,
    lvals_hbm,
    hidx,
    hcnt,
    hvals_hbm,
    srows,
    scnt,
    out_hbm,
    stat_ref,
    xb,
    xf,
    stage,
    outgoing,
    halo,
    lvals,
    hvals,
    wfull,
    bfull,
    tx,
    rx,
    tx2,
    acc,
    part,
    part_in,
    colpart,
    colpart_in,
    in_sem,
    halo_s,
    halo_r,
    w_s,
    w_r,
    wp_s,
    wp_r,
    b_s,
    b_r,
    p1_s,
    p1_r,
    p2_s,
    p2_r,
    own_sem,
    sd_s,
    sd_r,
    sc_s,
    sc_r,
):
    d = lax.axis_index("dom")
    z = lax.axis_index("col")
    rows, width = xf.shape
    slot_total = srows.shape[1]
    k_local = lvals.shape[1]
    k_halo = hvals.shape[1]
    f_total = weight_ref.shape[0]
    tiles_q = rows // TILE // n_col
    rows_q = tiles_q * TILE
    ct = CHUNK_TILES
    r_chunk = ct * TILE
    steps = tiles_q // ct
    per_peer = slot_total // TILE
    half = f_total // 2

    feat_copy = pltpu.make_async_copy(feat_hbm, xb, in_sem.at[0])
    feat_copy.start()

    barrier = pltpu.get_barrier_semaphore()
    for o in range(1, n_dom):
        pl.semaphore_signal(barrier, inc=1, device_id=(lax.rem(d + o, n_dom), z), device_id_type=MESH)
    for o in range(1, n_col):
        pl.semaphore_signal(barrier, inc=1, device_id=(d, lax.rem(z + o, n_col)), device_id_type=MESH)
    pl.semaphore_wait(barrier, n_dom - 1 + n_col - 1)

    core = lax.rem(d, 2)
    mate = d + 1 - 2 * core
    my_half = pl.ds(pl.multiple_of(core * half, half), half)

    def w_copy(o):
        return remote(
            weight_ref.at[my_half],
            wfull.at[z, my_half],
            w_s.at[o - 1],
            w_r.at[o - 1],
            (d, lax.rem(z + o, n_col)),
        )

    def w_pass(o):
        src = lax.rem(z + n_col - o, n_col)
        return remote(
            wfull.at[src, my_half], wfull.at[src, my_half], wp_s.at[o - 1], wp_r.at[o - 1], (mate, z)
        )

    def b_copy(o):
        return remote(
            bias_ref, bfull.at[z], b_s.at[o - 1], b_r.at[o - 1], (d, lax.rem(z + o, n_col))
        )

    for o in range(1, n_col):
        w_copy(o).start()
        b_copy(o).start()

    feat_copy.wait()
    lv_copy = pltpu.make_async_copy(lvals_hbm, lvals, in_sem.at[1])
    hv_copy = pltpu.make_async_copy(hvals_hbm, hvals, in_sem.at[2])
    lv_copy.start()
    hv_copy.start()

    @pl.loop(0, rows // TILE)
    def _(i):
        at = pl.ds(pl.multiple_of(i * TILE, TILE), TILE)
        xf[at, :] = xb[i].astype(jnp.float32)

    def halo_copy(o):
        return remote(
            outgoing.at[o],
            halo.at[pl.ds(d * per_peer, per_peer)],
            halo_s.at[o],
            halo_r.at[o],
            (lax.rem(d + o, n_dom), z),
        )

    @pl.loop(1, n_dom)
    def _(o):
        peer = lax.rem(d + o, n_dom)

        @pl.loop(0, slot_total // 16)
        def _(g):
            for k in range(16):
                at = g * 16 + k
                stage[at] = xf[srows[peer, at]]

        used = lax.broadcasted_iota(jnp.int32, (slot_total, width), 0) < scnt[0, peer]
        sent = jnp.where(used, stage[...], 0.0).astype(outgoing.dtype)
        outgoing[o] = sent.reshape(slot_total // TILE, TILE, width)
        halo_copy(o).start()

    halo[pl.ds(d * per_peer, per_peer)] = jnp.zeros((per_peer, TILE, width), halo.dtype)
    wfull[z] = weight_ref[...]
    bfull[z] = bias_ref[...]

    for o in range(1, n_col):
        w_copy(o).wait_recv()
        w_pass(o).start()

    lv_copy.wait()
    hv_copy.wait()

    @pl.loop(1, n_dom)
    def _(o):
        halo_copy(o).wait()

    def kept(count, k):
        one = jnp.minimum(jnp.maximum(count - k, 0), 1).astype(jnp.float32)
        return jnp.broadcast_to(one, (TILE, TILE)).astype(jnp.bfloat16)

    def tile_rows(t):
        lhs, rhs = [], []
        n_loc, n_hal = lcnt[0, t], hcnt[0, t]
        for k in range(k_local):
            v = lvals[t, k]
            lhs.append(v * kept(n_loc, k))
            rhs.append(xb[lidx[t, k]])
        for k in range(k_halo):
            v = hvals[t, k]
            lhs.append(v * kept(n_hal, k))
            rhs.append(halo[hidx[t, k]])
        total = jnp.dot(
            jnp.concatenate(lhs, axis=1),
            jnp.concatenate(rhs, axis=0),
            preferred_element_type=jnp.float32,
        )
        return total.astype(jnp.bfloat16)

    my_cols = pl.ds(pl.multiple_of(z * width, width), width)

    def p1_copy(s, o):
        return remote(
            tx.at[s, o - 1],
            rx.at[s, :, my_cols],
            p1_s.at[s, o - 1],
            p1_r.at[s, o - 1],
            (d, lax.rem(z + o, n_col)),
        )

    @pl.loop(0, steps)
    def _(s):
        for o in range(1, n_col):
            q = lax.rem(z + o, n_col)
            for c in range(ct):
                tx[s, o - 1, c * TILE : (c + 1) * TILE, :] = tile_rows(q * tiles_q + s * ct + c)
            p1_copy(s, o).start()
        for c in range(ct):
            rx[s, c * TILE : (c + 1) * TILE, my_cols] = tile_rows(z * tiles_q + s * ct + c)

    for o in range(1, n_col):
        w_pass(o).wait()
        b_copy(o).wait()
        w_copy(o).wait_send()

    acc[...] = jnp.zeros_like(acc)

    def out_rows(s):
        return pl.ds(pl.multiple_of(z * rows_q + s * r_chunk, r_chunk), r_chunk)

    def p2_copy(s, o):
        q = lax.rem(z + o, n_col)
        return remote(
            tx2.at[s, q],
            out_hbm.at[out_rows(s)],
            p2_s.at[s, o - 1],
            p2_r.at[s, o - 1],
            (d, q),
        )

    def own_copy(s):
        return pltpu.make_async_copy(tx2.at[s, z], out_hbm.at[out_rows(s)], own_sem.at[s])

    @pl.loop(0, steps)
    def _(s):
        for o in range(1, n_col):
            p1_copy(s, o).wait_recv()
        power = jnp.zeros((r_chunk, 1), jnp.float32)
        active = []
        for j in range(n_col):
            y = jnp.dot(rx[s], wfull[j], preferred_element_type=jnp.float32)
            y = jnp.maximum(y + bfull[j][0:1, :].astype(jnp.float32), 0.0)
            power = power + jnp.sum(y * y, axis=1, keepdims=True)
            active.append(y)
        factor = lax.rsqrt(power / f_total + epsilon)
        for j in range(n_col):
            scaled = active[j] * factor
            tx2[s, j] = scaled.astype(jnp.bfloat16)
            grouped = scaled.reshape(r_chunk // 8, 8, width)
            acc[j, 0] += jnp.sum(grouped, axis=0)
            acc[j, 1] += jnp.sum(grouped * grouped, axis=0)
        for o in range(1, n_col):
            p2_copy(s, o).start()
        own_copy(s).start()

    for j in range(n_col):
        part[j] = jnp.concatenate(
            [
                jnp.sum(acc[j, 0], axis=0, keepdims=True),
                jnp.sum(acc[j, 1], axis=0, keepdims=True),
                jnp.zeros((6, width), jnp.float32),
            ],
            axis=0,
        )

    def sd_copy(o):
        return remote(part, part_in.at[o], sd_s.at[o], sd_r.at[o], (lax.rem(d + o, n_dom), z))

    @pl.loop(1, n_dom)
    def _(o):
        sd_copy(o).start()

    part_in[0] = part[...]

    @pl.loop(1, n_dom)
    def _(o):
        sd_copy(o).wait()

    colpart[...] = jnp.sum(part_in[...], axis=0)

    def sc_copy(o):
        q = lax.rem(z + o, n_col)
        return remote(colpart.at[q], colpart_in.at[o], sc_s.at[o - 1], sc_r.at[o - 1], (d, q))

    for o in range(1, n_col):
        sc_copy(o).start()
    colpart_in[0] = colpart[z]

    @pl.loop(0, steps)
    def _(s):
        for o in range(1, n_col):
            p1_copy(s, o).wait_send()
            p2_copy(s, o).wait()
        own_copy(s).wait()

    for o in range(1, n_col):
        sc_copy(o).wait()
    totals = jnp.sum(colpart_in[...], axis=0) / node_total
    mean = totals[0:1, :]
    stat_ref[...] = jnp.concatenate([mean, totals[1:2, :] - mean * mean], axis=0)


def on_device(
    features,
    weight,
    out_bias,
    local_index,
    local_count,
    local_vals,
    halo_index,
    halo_count,
    halo_vals,
    send_rows,
    send_count,
):
    rows, width = features.shape
    n_dom = lax.axis_size("dom")
    n_col = lax.axis_size("col")
    slot_total = send_rows.shape[2]
    f_total = weight.shape[0]
    steps = rows // TILE // n_col // CHUNK_TILES
    r_chunk = CHUNK_TILES * TILE
    bias_rows = jnp.broadcast_to(out_bias[None, :], (16, width))
    any_spec = pl.BlockSpec(memory_space=pl.ANY)
    vmem = pl.BlockSpec(memory_space=pltpu.VMEM)
    smem = pl.BlockSpec(memory_space=pltpu.SMEM)
    bf16, f32 = jnp.bfloat16, jnp.float32
    dma = pltpu.SemaphoreType.DMA
    normalized, stats = pl.pallas_call(
        functools.partial(kernel, n_dom, n_col, rows * n_dom),
        out_shape=(
            jax.ShapeDtypeStruct((rows, width), bf16),
            jax.ShapeDtypeStruct((2, width), f32),
        ),
        in_specs=[any_spec, vmem, vmem, smem, smem, any_spec, smem, smem, any_spec, smem, smem],
        out_specs=(any_spec, vmem),
        scratch_shapes=[
            pltpu.VMEM((rows // TILE, TILE, width), bf16),
            pltpu.VMEM((rows, width), f32),
            pltpu.VMEM((slot_total, width), f32),
            pltpu.VMEM((n_dom, slot_total // TILE, TILE, width), bf16),
            pltpu.VMEM((n_dom * slot_total // TILE, TILE, width), bf16),
            pltpu.VMEM(local_vals.shape[1:], bf16),
            pltpu.VMEM(halo_vals.shape[1:], bf16),
            pltpu.VMEM((n_col, f_total, width), bf16),
            pltpu.VMEM((n_col, 16, width), bf16),
            pltpu.VMEM((steps, n_col - 1, r_chunk, width), bf16),
            pltpu.VMEM((steps, r_chunk, n_col * width), bf16),
            pltpu.VMEM((steps, n_col, r_chunk, width), bf16),
            pltpu.VMEM((n_col, 2, 8, width), f32),
            pltpu.VMEM((n_col, 8, width), f32),
            pltpu.VMEM((n_dom, n_col, 8, width), f32),
            pltpu.VMEM((n_col, 8, width), f32),
            pltpu.VMEM((n_col, 8, width), f32),
            dma((3,)),
            dma((n_dom,)),
            dma((n_dom,)),
            dma((n_col - 1,)),
            dma((n_col - 1,)),
            dma((n_col - 1,)),
            dma((n_col - 1,)),
            dma((n_col - 1,)),
            dma((n_col - 1,)),
            dma((steps, n_col - 1)),
            dma((steps, n_col - 1)),
            dma((steps, n_col - 1)),
            dma((steps, n_col - 1)),
            dma((steps,)),
            dma((n_dom,)),
            dma((n_dom,)),
            dma((n_col - 1,)),
            dma((n_col - 1,)),
        ],
        compiler_params=pltpu.CompilerParams(
            collective_id=0, has_side_effects=True, vmem_limit_bytes=67043328
        ),
    )(
        features.reshape(rows // TILE, TILE, width),
        weight,
        bias_rows,
        local_index[0],
        local_count,
        local_vals[0],
        halo_index[0],
        halo_count,
        halo_vals[0],
        send_rows[0],
        send_count,
    )
    return normalized, stats


def solution(mesh):
    in_specs = (
        P("dom", "col"),
        P(None, "col"),
        P("col"),
        P("dom", None, None),
        P("dom", None),
        P("dom", None, None, None, None),
        P("dom", None, None),
        P("dom", None),
        P("dom", None, None, None, None),
        P("dom", None, None),
        P("dom", None),
    )
    out_specs = (P("dom", "col"), P(None, "col"))
    return jax.shard_map(
        on_device, mesh=mesh, in_specs=in_specs, out_specs=out_specs, check_vma=False
    )
```

time: 375 us -> 233 us (0.62); the launches traced: 375 us -> 229 us
  Pallas kernels: 0 us -> 219 us
  blocking collectives: 218 us -> 0 us
  local copies, waits for them, and re-layouts: 50.3 us -> 9.07 us
  matrix products: 35.5 us -> 0 us
  waiting for transfers between devices: 34.4 us -> 0 us
  starting transfers between devices: 14.9 us -> 0 us
  between operations: 14.2 us -> 0.65 us
  other arithmetic: 7.48 us -> 0 us
    pallas_call x0 -> x1, Pallas kernels: none -> 219 us  [on_device(): pl.pallas_call(functools.partial(kernel, n_dom, n_col, rows * n_dom), out...]
    psum x1 -> x0, blocking collectives: 114 us -> none  [on_device(): lax.psum((jnp.sum(scaled, axis=0), jnp.sum(scaled * scaled, axis=0)), ('d...]
    all_gather x1 -> x0, blocking collectives: 104 us -> none  [on_device(): lax.all_gather(out_bias.reshape(1, col_width), 'col', axis=1, tiled=True)]
    gather x3 -> x0, local copies, waits for them, and re-layouts: 37.4 us -> none  [the longest x2 21.7 us: tile_sum(): gathered = sources[tile_index]]
    dot_general x3 -> x0, matrix products: 35.5 us -> none  [the longest x2 27.7 us: tile_sum(): jnp.einsum('tkij,tkjc->tic', masked, gathered, preferred_element_type=jnp...]
    all_to_all x3 -> x0, waiting for transfers between devices: 33.8 us -> none  [the longest x1 19.8 us: on_device(): lax.all_to_all(spread, 'col', split_axis=0, concat_axis=1, tiled=True)]
    all_to_all x3 -> x0, starting transfers between devices: 14.9 us -> none  [the longest x1 5.2 us: on_device(): lax.all_to_all(outgoing, 'dom', split_axis=0, concat_axis=0, tiled=True)]
    unnamed x12 -> x6, local copies, waits for them, and re-layouts: 0.04 us -> 7.82 us
  transfers between devices with their start and end apart: 4 -> 0, of which waited for: 2 -> 0; matrix products, arithmetic and copies ran while one was open for 4% -> 0% of each run, Pallas kernels for 0% -> 0%
where the time goes in v1:
time: 233 us; the launch traced here: 229 us
  Pallas kernels  219 us (94%)
  local copies, waits for them, and re-layouts  9.07 us (4%)
    pallas_call x1, Pallas kernels, on_device(): pl.pallas_call(functools.partial(kernel, n_dom, n_col, rows * n_dom), out...  219 us
    unnamed x6, local copies, waits for them, and re-layouts  7.82 us

profile of v1, /device:TPU:0, one launch (start us, length us, event | category | flops | bytes accessed | tf_op | source)
XLA Modules:
  0.0 228.9 jit_solution(12328574061402690308)
XLA Ops:
  0.6 1.2 broadcast_in_dim.2.bias_ref
  1.9 1.4 copy.13
  3.3 1.4 copy.14
  4.6 219.1 %shard_map.122 = (bf16[8192,256]{1,0:T(8,128)(2,1)}, f32[2,256]{1,0:T(2,128)}) custom-call(bf16[64,128,256]{2,1,0:T(8,128)(2,1)} %bitcast.8, bf16[1024,256]{1,0:T(8,128)(2,1)} %weight_ref.1, bf16[16,256]{1,0:T(8,128)(2,1)} %broadcast_in_dim.2.bias_ref, s32[64,4]{1,0:T(8,128)} %bitcast.9, s32[1,64]{1,0:T(1,128)} %lcnt.1, bf16[64,4,128,128]{3,2,1,0:T(8,128)(2,1)} %bitcast.6, ...), custom_call_target="tpu_custom_call" | custom-call | tf_op jit(solution)/shard_map/pallas_call | solution.py:344
  223.8 0.0 copy-start
  223.8 4.5 %copy.17 = bf16[8192,256]{1,0:T(8,128)(2,1)} copy(bf16[8192,256]{1,0:T(8,128)(2,1)} %get-tuple-element.4) | data formatting | bytes 8388608
  228.3 0.0 copy-done
  228.3 0.6 copy.18
Async XLA Ops:
  223.8 4.5 %copy-start = (f32[2,256]{1,0:T(2,128)S(1)}, f32[2,256]{1,0:T(2,128)}, u32[]{:S(2)}) copy-start(f32[2,256]{1,0:T(2,128)} %get-tuple-element.5) | copy-start | bytes 6148

commit v2 on v1

--- a/solution.py
+++ b/solution.py
@@ -92,8 +92,16 @@
     per_peer = slot_total // TILE
     half = f_total // 2
 
-    feat_copy = pltpu.make_async_copy(feat_hbm, xb, in_sem.at[0])
-    feat_copy.start()
+    pieces = in_sem.shape[0] - 2
+    piece = rows // TILE // pieces
+
+    def feat_copy(i):
+        at = pl.ds(i * piece, piece)
+        return pltpu.make_async_copy(feat_hbm.at[at], xb.at[at], in_sem.at[2 + i])
+
+    for i in range(pieces):
+        feat_copy(i).start()
+    bfull[z] = jnp.broadcast_to(bias_ref[...], bfull.shape[1:])
 
     barrier = pltpu.get_barrier_semaphore()
     for o in range(1, n_dom):
@@ -123,23 +131,27 @@
 
     def b_copy(o):
         return remote(
-            bias_ref, bfull.at[z], b_s.at[o - 1], b_r.at[o - 1], (d, lax.rem(z + o, n_col))
+            bfull.at[z], bfull.at[z], b_s.at[o - 1], b_r.at[o - 1], (d, lax.rem(z + o, n_col))
         )
 
     for o in range(1, n_col):
         w_copy(o).start()
-        b_copy(o).start()
-
-    feat_copy.wait()
-    lv_copy = pltpu.make_async_copy(lvals_hbm, lvals, in_sem.at[1])
-    hv_copy = pltpu.make_async_copy(hvals_hbm, hvals, in_sem.at[2])
+
+    lv_copy = pltpu.make_async_copy(lvals_hbm, lvals, in_sem.at[0])
+    hv_copy = pltpu.make_async_copy(hvals_hbm, hvals, in_sem.at[1])
     lv_copy.start()
     hv_copy.start()
 
-    @pl.loop(0, rows // TILE)
+    @pl.loop(0, pieces)
     def _(i):
-        at = pl.ds(pl.multiple_of(i * TILE, TILE), TILE)
-        xf[at, :] = xb[i].astype(jnp.float32)
+        feat_copy(i).wait()
+        for j in range(piece):
+            t = i * piece + j
+            at = pl.ds(pl.multiple_of(t * TILE, TILE), TILE)
+            xf[at, :] = xb[t].astype(jnp.float32)
+
+    def peer_of(o):
+        return lax.rem(d + (1 - 2 * core) * o + n_dom, n_dom)
 
     def halo_copy(o):
         return remote(
@@ -147,12 +159,13 @@
             halo.at[pl.ds(d * per_peer, per_peer)],
             halo_s.at[o],
             halo_r.at[o],
-            (lax.rem(d + o, n_dom), z),
-        )
-
-    @pl.loop(1, n_dom)
-    def _(o):
-        peer = lax.rem(d + o, n_dom)
+            (peer_of(o), z),
+        )
+
+    @pl.loop(0, n_dom - 1)
+    def _(i):
+        o = lax.rem(i + 1, n_dom - 1) + 1
+        peer = peer_of(o)
 
         @pl.loop(0, slot_total // 16)
         def _(g):
@@ -167,11 +180,11 @@
 
     halo[pl.ds(d * per_peer, per_peer)] = jnp.zeros((per_peer, TILE, width), halo.dtype)
     wfull[z] = weight_ref[...]
-    bfull[z] = bias_ref[...]
 
     for o in range(1, n_col):
         w_copy(o).wait_recv()
         w_pass(o).start()
+        b_copy(o).start()
 
     lv_copy.wait()
     hv_copy.wait()
@@ -190,11 +203,11 @@
         for k in range(k_local):
             v = lvals[t, k]
             lhs.append(v * kept(n_loc, k))
-            rhs.append(xb[lidx[t, k]])
+            rhs.append(xb[lidx[k, t]])
         for k in range(k_halo):
             v = hvals[t, k]
             lhs.append(v * kept(n_hal, k))
-            rhs.append(halo[hidx[t, k]])
+            rhs.append(halo[hidx[k, t]])
         total = jnp.dot(
             jnp.concatenate(lhs, axis=1),
             jnp.concatenate(rhs, axis=0),
@@ -335,7 +348,6 @@
     f_total = weight.shape[0]
     steps = rows // TILE // n_col // CHUNK_TILES
     r_chunk = CHUNK_TILES * TILE
-    bias_rows = jnp.broadcast_to(out_bias[None, :], (16, width))
     any_spec = pl.BlockSpec(memory_space=pl.ANY)
     vmem = pl.BlockSpec(memory_space=pltpu.VMEM)
     smem = pl.BlockSpec(memory_space=pltpu.SMEM)
@@ -367,7 +379,7 @@
             pltpu.VMEM((n_dom, n_col, 8, width), f32),
             pltpu.VMEM((n_col, 8, width), f32),
             pltpu.VMEM((n_col, 8, width), f32),
-            dma((3,)),
+            dma((10 if rows // TILE % 8 == 0 else 3,)),
             dma((n_dom,)),
             dma((n_dom,)),
             dma((n_col - 1,)),
@@ -392,11 +404,11 @@
     )(
         features.reshape(rows // TILE, TILE, width),
         weight,
-        bias_rows,
-        local_index[0],
+        out_bias.reshape(1, width),
+        local_index[0].T,
         local_count,
         local_vals[0],
-        halo_index[0],
+        halo_index[0].T,
         halo_count,
         halo_vals[0],
         send_rows[0],

time: 233 us -> 229 us (0.983); the launches traced: 229 us -> 229 us
  Pallas kernels: 219 us -> 222 us
  local copies, waits for them, and re-layouts: 9.07 us -> 6.27 us
    pallas_call x1, Pallas kernels: 219 us -> 222 us  [on_device(): pl.pallas_call(functools.partial(kernel, n_dom, n_col, rows * n_dom), out...]
    unnamed x6 -> x4, local copies, waits for them, and re-layouts: 7.82 us -> 5.05 us
where the time goes in v2:
time: 229 us
  Pallas kernels  222 us (97%)
  local copies, waits for them, and re-layouts  6.27 us (3%)
    pallas_call x1, Pallas kernels, on_device(): pl.pallas_call(functools.partial(kernel, n_dom, n_col, rows * n_dom), out...  222 us
    unnamed x4, local copies, waits for them, and re-layouts  5.05 us

profile of v2, /device:TPU:0, one launch (start us, length us, event | category | flops | bytes accessed | tf_op | source)
XLA Modules:
  0.0 229.2 jit_solution(4240193806779838181)
XLA Ops:
  0.6 1.2 reshape.11.bias_ref
  1.9 222.3 %shard_map.122 = (bf16[8192,256]{1,0:T(8,128)(2,1)}, f32[2,256]{1,0:T(2,128)}) custom-call(bf16[64,128,256]{2,1,0:T(8,128)(2,1)} %bitcast.12, bf16[1024,256]{1,0:T(8,128)(2,1)} %weight_ref.1, bf16[1,256]{1,0:T(2,128)(2,1)} %reshape.11.bias_ref, s32[4,64]{1,0:T(4,128)} %bitcast.14, s32[1,64]{1,0:T(1,128)} %lcnt.1, bf16[64,4,128,128]{3,2,1,0:T(8,128)(2,1)} %bitcast.10, ...), custom_call_target="tpu_custom_call" | custom-call | tf_op jit(solution)/shard_map/pallas_call | solution.py:356
  224.1 0.0 copy-start
  224.1 4.5 %copy.15 = bf16[8192,256]{1,0:T(8,128)(2,1)} copy(bf16[8192,256]{1,0:T(8,128)(2,1)} %get-tuple-element.4) | data formatting | bytes 8388608
  228.6 0.0 copy-done
  228.6 0.6 copy.16
Async XLA Ops:
  224.1 4.5 %copy-start = (f32[2,256]{1,0:T(2,128)S(1)}, f32[2,256]{1,0:T(2,128)}, u32[]{:S(2)}) copy-start(f32[2,256]{1,0:T(2,128)} %get-tuple-element.5) | copy-start | bytes 6148
